TPU v7x, 32 devices: a whole 2x2x4 slice. The times are simulated.
32 devices in a mesh: blk: 8 (over z, x), rep: 4 (over y, core).
Axes of the slice: x: 2, y: 2, z: 4, core: 2. Of those that a mesh axis runs over, the one named last changes fastest.
Arguments:
- query_embed: bfloat16 [8, 4, 256, 256], P('blk', 'rep'), may hold values from -96 to 96
- positive_ids: int32 [8, 4, 256], P('blk'), may hold values from 0 to 2047, as said below
- pair_blocks: int32 [8, 8], P('blk'), may hold values from 0 to 31, as said below
- code_ids: int32 [8, 4, 8, 64], P('blk', 'rep'), may hold values from 0 to 255
- codebooks: bfloat16 [2048, 256], replicated, may hold values from -3 to 3
Outputs:
- query_loss: float32 [8, 4, 256], P('blk', 'rep')
- query_grad: float32 [8, 4, 256, 256], P('blk', 'rep')
- passage_grad: float32 [8, 4, 64, 256], P('blk', 'rep')
- codebook_grad: float32 [2048, 256], P(('blk', 'rep'))
Inputs may be any that keep to these rules, and one draw needn't show every extreme that they name: `pair_blocks`: each row names 8 different passage blocks; at most 2 of them belong to one owner o (blocks o * 4 to o * 4 + 3), and in every row some owner has exactly 2. Some blocks are named in many rows. `positive_ids`: the positive passage of a query lies in a block named in its query block's row of pair_blocks.
All inputs are finite; a program needn't handle non-finite values.
Results may differ from a plain program's by a relative error of at most 0.0079.
Values may be sent and summed in bfloat16 or wider, within the bound.
A program may use at most 64 MiB of HBM per device.

v0:
```python
import jax
import jax.numpy as jnp
from jax import lax
from jax.sharding import PartitionSpec as P

CODES = 256
PR = 16
PBLK_DEV = 4
CAP = 2


EPS = 1e-06


def joined(x, axis, combine):
    everything = jax.tree.map(lambda part: lax.all_gather(part, axis), x)
    initial = jax.tree.map(lambda part: part[0], everything)

    def lap(k, so_far):
        return combine(so_far, jax.tree.map(lambda part: part[k], everything))

    return lax.fori_loop(1, lax.axis_size(axis), lap, initial)


def unit_rows(local_codes, codebooks):
    book_total = local_codes.shape[0]
    table_rows = codebooks.shape[0] // book_total
    code_iota = jnp.arange(table_rows, dtype=jnp.int32)
    pieces = []
    for book_index in range(book_total):
        pieces.append((local_codes[book_index][:, None] == code_iota[None, :]).astype(jnp.bfloat16))
    onehot = jnp.concatenate(pieces, axis=1)
    quant = jnp.dot(onehot, codebooks, preferred_element_type=jnp.float32)
    inverse = lax.rsqrt(jnp.sum(quant * quant, axis=1, keepdims=True) + EPS)
    return (quant * inverse, inverse)


def group_view(blocks):
    pair_count, span_rows, feat_count = blocks.shape
    group_size = min(8, pair_count)
    return blocks.reshape(pair_count // group_size, group_size * span_rows, feat_count)


def score_block(row_block, group_rows):
    return lax.dot_general(
        row_block, group_rows, (((1,), (1,)), ((), ())), preferred_element_type=jnp.float32
    )


def column_stats(row_block, grouped, target_col):
    row_count = row_block.shape[0]
    span_cols = grouped.shape[1]
    column_iota = jnp.arange(span_cols, dtype=jnp.int32)

    def visit(carry, item):
        peak_old, total_old, hit_old = carry
        group_index, group_rows = item
        scores = score_block(row_block, group_rows)
        peak_new = jnp.maximum(peak_old, jnp.max(scores, axis=1))
        total_new = total_old * jnp.exp(peak_old - peak_new) + jnp.sum(
            jnp.exp(scores - peak_new[:, None]), axis=1
        )
        here_cols = group_index * span_cols + column_iota
        hit_new = hit_old + jnp.sum(
            jnp.where(here_cols[None, :] == target_col[:, None], scores, 0.0), axis=1
        )
        return ((peak_new, total_new, hit_new), None)

    start = (
        jnp.full((row_count,), -1e30, jnp.float32),
        jnp.zeros((row_count,), jnp.float32),
        jnp.zeros((row_count,), jnp.float32),
    )
    group_ids = jnp.arange(grouped.shape[0], dtype=jnp.int32)
    result, unused = lax.scan(visit, start, (group_ids, grouped))
    return result


def column_grads(row_block, grouped, target_col, lse):
    span_cols = grouped.shape[1]
    column_iota = jnp.arange(span_cols, dtype=jnp.int32)

    def visit(grad_rows, item):
        group_index, group_rows = item
        scores = score_block(row_block, group_rows)
        here_cols = group_index * span_cols + column_iota
        hit_mask = (here_cols[None, :] == target_col[:, None]).astype(jnp.float32)
        weight = (jnp.exp(scores - lse[:, None]) - hit_mask).astype(jnp.bfloat16)
        grad_rows = grad_rows + jnp.dot(weight, group_rows, preferred_element_type=jnp.float32)
        grad_cols = lax.dot_general(
            weight, row_block, (((0,), (0,)), ((), ())), preferred_element_type=jnp.float32
        )
        return (grad_rows, grad_cols)

    start = jnp.zeros((row_block.shape[0], row_block.shape[1]), jnp.float32)
    group_ids = jnp.arange(grouped.shape[0], dtype=jnp.int32)
    return lax.scan(visit, start, (group_ids, grouped))


def merge_partials(first, second):
    peak_both = jnp.maximum(first[0], second[0])
    total_both = first[1] * jnp.exp(first[0] - peak_both) + second[1] * jnp.exp(
        second[0] - peak_both
    )
    return (peak_both, total_both, first[2] + second[2])


def find_slot(wanted, target_block):
    slot_iota = jnp.arange(wanted.shape[0], dtype=jnp.int32)
    return jnp.sum(
        jnp.where(wanted[None, :] == target_block[:, None], slot_iota[None, :], 0), axis=1
    )


def shards(query_embed, positive_ids, pair_blocks, code_ids, codebooks):
    rep_count = lax.axis_size("rep")
    here_blk = lax.axis_index("blk")
    here_rep = lax.axis_index("rep")
    rows_mine = query_embed[0, 0]
    wanted = pair_blocks[0]
    pair_count = wanted.shape[0]
    feat_count = rows_mine.shape[1]
    block_rows = PR * rep_count
    local_codes = code_ids[0, 0]
    unit, inverse = unit_rows(local_codes, codebooks)
    unit_bf = unit.astype(jnp.bfloat16)
    directory = lax.all_gather(pair_blocks, "blk", axis=0, tiled=True)
    owner_count = directory.shape[0]
    local_iota = jnp.arange(PBLK_DEV, dtype=jnp.int32)
    named = jnp.sum(
        (directory[:, :, None] == here_blk * PBLK_DEV + local_iota[None, None, :]).astype(
            jnp.int32
        ),
        axis=1,
    )
    earlier_named = jnp.cumsum(named, axis=1) - named
    cap_iota = jnp.arange(CAP, dtype=jnp.int32)
    selector = (named[:, None, :] > 0) & (earlier_named[:, None, :] == cap_iota[None, :, None])
    outbound = jnp.einsum(
        "bkj,jie->bkie",
        selector.astype(jnp.bfloat16),
        unit_bf.reshape(PBLK_DEV, PR, feat_count),
        preferred_element_type=jnp.float32,
    ).astype(jnp.bfloat16)
    arrived = lax.all_to_all(outbound, "blk", split_axis=0, concat_axis=0, tiled=True)
    owner_of = wanted // PBLK_DEV
    within_of = wanted % PBLK_DEV
    before_me = jnp.sum(
        (
            (owner_of[None, :] == owner_of[:, None]) & (within_of[None, :] < within_of[:, None])
        ).astype(jnp.int32),
        axis=1,
    )
    slot_index = owner_of * CAP + before_me
    fetched = jnp.take(arrived.reshape(owner_count * CAP, PR, feat_count), slot_index, axis=0)
    every_row = lax.all_gather(rows_mine, "rep", axis=0, tiled=True)
    all_targets = positive_ids[0].reshape(-1)
    row_in = all_targets % block_rows
    target_slot = find_slot(wanted, all_targets // block_rows)
    target_col = jnp.where(row_in // PR == here_rep, target_slot * PR + row_in % PR, -1)
    grouped = group_view(fetched)
    partial_stats = column_stats(every_row, grouped, target_col)
    peak_all, total_all, hit_all = joined(partial_stats, "rep", merge_partials)
    lse = peak_all + jnp.log(total_all)
    query_loss = lax.dynamic_slice_in_dim(
        lse - hit_all, here_rep * rows_mine.shape[0], rows_mine.shape[0]
    )
    grad_rows, grad_cols = column_grads(every_row, grouped, target_col, lse)
    query_grad = lax.psum_scatter(grad_rows, "rep", scatter_dimension=0, tiled=True)
    quarter_grad = grad_cols.reshape(pair_count, PR, feat_count)
    backward = (
        jnp.zeros((owner_count * CAP, PR, feat_count), jnp.float32).at[slot_index].set(quarter_grad)
    )
    returned = lax.all_to_all(
        backward.reshape(owner_count, CAP, PR, feat_count),
        "blk",
        split_axis=0,
        concat_axis=0,
        tiled=True,
    )
    unit_grad = jnp.einsum(
        "bkj,bkie->jie", selector.astype(jnp.float32), returned, precision=lax.Precision.HIGHEST
    ).reshape(PBLK_DEV * PR, feat_count)
    passage_grad = inverse * (unit_grad - unit * jnp.sum(unit * unit_grad, axis=1, keepdims=True))
    share_rows = codebooks.shape[0] // (owner_count * rep_count)
    row_ids = jnp.arange(lax.axis_size(("blk", "rep")) * share_rows, dtype=jnp.int32)
    book_of = row_ids // CODES
    code_of = row_ids % CODES
    picked = jnp.take(local_codes, book_of, axis=0)
    member = (picked == code_of[:, None]).astype(jnp.float32)
    codebook_grad = lax.psum_scatter(
        jnp.dot(member, passage_grad, precision=lax.Precision.HIGHEST),
        ("blk", "rep"),
        scatter_dimension=0,
        tiled=True,
    )
    return (query_loss[None, None], query_grad[None, None], passage_grad[None, None], codebook_grad)


def solution(mesh):
    placed = (
        P("blk", "rep", None, None),
        P("blk", None, None),
        P("blk", None),
        P("blk", "rep", None, None),
        P(),
    )
    return jax.shard_map(
        shards,
        mesh=mesh,
        in_specs=placed,
        out_specs=(
            P("blk", "rep", None),
            P("blk", "rep", None, None),
            P("blk", "rep", None, None),
            P(("blk", "rep"), None),
        ),
        check_vma=False,
    )
```

profile of v0, /device:TPU:0, one launch (start us, length us, event | category | flops | bytes accessed | tf_op | source)
XLA Modules:
  0.0 236.5 jit_solution(8785457381588116860)
XLA Ops:
  7.2 22.6 %all-gather.3 = s32[8,1,8]{2,1,0:T(1,128)S(1)} all-gather(s32[1,1,8]{2,1,0:T(1,128)} %bitcast.140), channel_id=1, replica_groups=mesh['blk'=8,'rep'=4] {'blk'}, dimensions={0}, use_global_device_ids=true | all-gather | bytes 288 | tf_op jit(solution)/shard_map/all_gather | solution.py:127
  29.8 0.2 convert_reduce_fusion
  30.1 1.0 slice_bitcast_fusion
  31.8 0.4 multiply_reduce_fusion
  32.2 0.2 convolution_convert_fusion
  32.5 0.7 copy.21
  33.2 3.4 %all-to-all-start = ((bf16[8,2,16,256]{3,2,1,0:T(8,128)(2,1)}), bf16[8,2,16,256]{3,2,1,0:T(8,128)(2,1)S(1)}, u32[]{:S(2)}, u32[]{:S(2)}) async-start(bf16[8,2,16,256]{3,2,1,0:T(8,128)(2,1)} %copy.21), calls=%async_computation | async-start | bytes 262144 | tf_op jit(solution)/shard_map/all_to_all | solution.py:145
  36.6 0.2 convert_reduce_fusion.1
  36.9 7.2 %all-gather = bf16[1,1,1024,256]{3,2,1,0:T(8,128)(2,1)S(1)} all-gather(bf16[1,1,256,256]{3,2,1,0:T(8,128)(2,1)S(1)} %copy-done.3), channel_id=2, replica_groups=mesh['blk'=8,'rep'=4] {'rep'}, dimensions={2}, use_global_device_ids=true | all-gather | bytes 655360 | tf_op jit(solution)/shard_map/all_gather | solution.py:156
  44.3 0.1 broadcast_in_dim.102
  44.4 0.6 gather_fusion
  44.9 0.1 bitcast_select_fusion.1
  45.0 0.3 fusion.61
  45.4 0.1 fusion.3
  45.5 5.2 %all-gather.4 = f32[4,1,1024]{2,1,0:T(1,128)S(1)} all-gather(f32[1,1,1024]{2,1,0:T(1,128)S(1)} %bitcast.137), channel_id=1, replica_groups=mesh['blk'=8,'rep'=4] {'rep'}, dimensions={0}, use_global_device_ids=true | all-gather | bytes 20480 | tf_op jit(solution)/shard_map/all_gather | solution.py:16
  50.7 5.2 %all-gather.2 = f32[4096]{0:T(1024)S(1)} all-gather(f32[1024]{0:T(1024)S(1)} %get-tuple-element.233), channel_id=4, replica_groups=mesh['blk'=8,'rep'=4] {'rep'}, dimensions={0}, use_global_device_ids=true | all-gather | bytes 20480 | tf_op jit(solution)/shard_map/all_gather | solution.py:16
  56.0 5.2 %all-gather.1 = f32[4096]{0:T(1024)S(1)} all-gather(f32[1024]{0:T(1024)S(1)} %broadcast_maximum_fusion), channel_id=3, replica_groups=mesh['blk'=8,'rep'=4] {'rep'}, dimensions={0}, use_global_device_ids=true | all-gather | bytes 20480 | tf_op jit(solution)/shard_map/all_gather | solution.py:16
  61.2 0.3 while.12
  61.5 1.3 fusion.47
  62.8 0.3 fusion.7
  63.1 0.7 scatter_fusion
  63.9 0.9 copy.22
  64.8 5.9 %all-to-all-start.1 = ((f32[8,2,16,256]{3,1,2,0:T(2,128)}), f32[8,2,16,256]{3,1,2,0:T(2,128)S(1)}, u32[]{:S(2)}, u32[]{:S(2)}) async-start(f32[8,2,16,256]{3,1,2,0:T(2,128)} %copy.22), calls=%async_computation.2 | async-start | bytes 524288 | tf_op jit(solution)/shard_map/all_to_all | solution.py:174
  70.7 5.5 %gather_fusion.1 = s32[2048,64]{1,0:T(8,128)S(1)} fusion(s32[8,64]{1,0:T(8,128)S(1)} %bitcast.123, s32[2048]{0:T(1024)S(1)} %broadcast_clamp_fusion), kind=kCustom, calls=%fused_computation.1 | custom fusion | bytes 1056768 | tf_op jit(solution)/shard_map/jit(_take)/gather | solution.py:189
  76.2 3.9 %all-to-all-done.1 = f32[8,2,16,256]{3,1,2,0:T(2,128)S(1)} async-done(((f32[8,2,16,256]{3,1,2,0:T(2,128)}), f32[8,2,16,256]{3,1,2,0:T(2,128)S(1)}, u32[]{:S(2)}, u32[]{:S(2)}) %all-to-all-start.1) | async-done | bytes 262176 | tf_op jit(solution)/shard_map/all_to_all | solution.py:174
  80.1 0.4 convolution_bitcast_fusion
  80.5 0.2 fusion.15
  80.6 0.1 fusion.16
  80.8 3.3 %fusion = f32[2048,256]{1,0:T(8,128)} fusion(f32[64,256]{1,0:T(8,128)S(1)} %fusion.16, s32[2048,64]{1,0:T(8,128)S(1)} %gather_fusion.1, s32[2048]{0:T(1024)S(1)} %fusion.27, pred[2048]{0:T(1024)(128)(4,1)S(1)} %fusion.36), kind=kOutput, calls=%fused_computation.10 | convolution fusion | flops 402915328 | bytes 2697216 | tf_op jit(solution)/shard_map/dot_general | solution.py:192
  84.1 0.6 dynamic_slice.43
  84.7 3.7 %reduce-scatter.3.cloned.1.call-done = f32[256,256]{1,0:T(8,128)} async-done(((f32[1024,256]{1,0:T(8,128)}), f32[256,256]{1,0:T(8,128)}) %reduce-scatter.3.cloned.1.call-update) | async-done | bytes 262160 | tf_op jit(solution)/shard_map/reduce_scatter | solution.py:169
  88.4 141.2 %reduce-scatter.5.cloned.1.call-done = f32[64,256]{1,0:T(8,128)} async-done(((f32[2048,256]{1,0:T(8,128)}), f32[64,256]{1,0:T(8,128)}) %reduce-scatter.5.cloned.1.call-update) | async-done | bytes 65552 | tf_op jit(solution)/shard_map/reduce_scatter | solution.py:191
  (68 shorter events, 1.4 us)
Async XLA Ops:
  7.2 24.6 %copy-start = (bf16[2048,256]{1,0:T(8,128)(2,1)S(1)}, bf16[2048,256]{1,0:T(8,128)(2,1)}, u32[]{:S(2)}) copy-start(bf16[2048,256]{1,0:T(8,128)(2,1)} %param.11) | copy-start | bytes 3145732
  7.2 29.4 %copy-start.5 = (s32[1,8]{1,0:T(1,128)S(1)}, s32[1,8]{1,0:T(1,128)}, u32[]{:S(2)}) copy-start(s32[1,8]{1,0:T(1,128)} %param.9) | copy-start | bytes 100
  7.2 29.7 %copy-start.4 = (s32[1,4,256]{2,1,0:T(4,128)S(1)}, s32[1,4,256]{2,1,0:T(4,128)}, u32[]{:S(2)}) copy-start(s32[1,4,256]{2,1,0:T(4,128)} %param.8) | copy-start | bytes 12292
  7.2 29.7 %copy-start.3 = (bf16[1,1,256,256]{3,2,1,0:T(8,128)(2,1)S(1)}, bf16[1,1,256,256]{3,2,1,0:T(8,128)(2,1)}, u32[]{:S(2)}) copy-start(bf16[1,1,256,256]{3,2,1,0:T(8,128)(2,1)} %param.7) | copy-start | bytes 393220
  33.2 11.2 %all-to-all-start = ((bf16[8,2,16,256]{3,2,1,0:T(8,128)(2,1)}), bf16[8,2,16,256]{3,2,1,0:T(8,128)(2,1)S(1)}, u32[]{:S(2)}, u32[]{:S(2)}) async-start(bf16[8,2,16,256]{3,2,1,0:T(8,128)(2,1)} %copy.21), calls=%async_computation | async-start | bytes 262144 | tf_op jit(solution)/shard_map/all_to_all | solution.py:145
  36.5 51.9 %reduce-scatter.3.cloned.1.call-start = ((), (), s32[]{:S(2)}) async-start(), calls=%async_computation.4 | async-start | bytes 1310720 | tf_op jit(solution)/shard_map/reduce_scatter | solution.py:169
  62.8 7.9 %copy-start.1 = (s32[1,1,8,64]{3,2,1,0:T(8,128)S(1)}, s32[1,1,8,64]{3,2,1,0:T(8,128)}, u32[]{:S(2)}) copy-start(s32[1,1,8,64]{3,2,1,0:T(8,128)} %param.10) | copy-start | bytes 6148
  64.8 15.3 %all-to-all-start.1 = ((f32[8,2,16,256]{3,1,2,0:T(2,128)}), f32[8,2,16,256]{3,1,2,0:T(2,128)S(1)}, u32[]{:S(2)}, u32[]{:S(2)}) async-start(f32[8,2,16,256]{3,1,2,0:T(2,128)} %copy.22), calls=%async_computation.2 | async-start | bytes 524288 | tf_op jit(solution)/shard_map/all_to_all | solution.py:174
  70.6 159.0 %reduce-scatter.5.cloned.1.call-start = ((), (), s32[]{:S(2)}) async-start(), calls=%async_computation.5 | async-start | bytes 2162688 | tf_op jit(solution)/shard_map/reduce_scatter | solution.py:191
  80.7 3.4 %copy-start.2 = (f32[64,256]{1,0:T(8,128)}, f32[64,256]{1,0:T(8,128)S(1)}, u32[]{:S(2)}) copy-start(f32[64,256]{1,0:T(8,128)S(1)} %fusion.16) | copy-start | bytes 196612
Sparse Core Ops, SparseCore 0:
  62.9 25.4 reduce-scatter.2
  91.2 138.3 reduce-scatter.4
where the time goes:
time: 237 us; the launch traced here: 236 us
  waiting for transfers between devices  149 us (63%)
  blocking collectives  45.4 us (19%)
  between operations  14.4 us (6%)
  local copies, waits for them, and re-layouts  10.3 us (4%)
  starting transfers between devices  9.33 us (4%)
  matrix products  6.19 us (3%)
    reduce_scatter x1, waiting for transfers between devices, shards(): lax.psum_scatter(jnp.dot(member, passage_grad, precision=lax.Precision.HI...  141 us
    all_gather x1, blocking collectives, shards(): directory = lax.all_gather(pair_blocks, 'blk', axis=0, tiled=True)  22.6 us
    all_gather x3, blocking collectives, joined(): everything = jax.tree.map(lambda part: lax.all_gather(part, axis), x)  15.6 us
    all_gather x1, blocking collectives, shards(): every_row = lax.all_gather(rows_mine, 'rep', axis=0, tiled=True)  7.2 us
    all_to_all x1, starting transfers between devices, shards(): lax.all_to_all(backward.reshape(owner_count, CAP, PR, feat_count), 'blk',...  5.88 us
    gather x1, local copies, waits for them, and re-layouts, shards(): picked = jnp.take(local_codes, book_of, axis=0)  5.46 us
  transfers between devices with their start and end apart: 4, of which 3 were waited for; matrix products, arithmetic and copies ran while one was open for 5% of the time, Pallas kernels for 0%

commit v1 on v0

v1 whole, which is shorter than its diff:
```python
import functools

import jax
import jax.numpy as jnp
from jax import lax
from jax.experimental import pallas as pl
from jax.experimental.pallas import tpu as pltpu
from jax.sharding import PartitionSpec as P

CODES = 256
PR = 16
PBLK_DEV = 4
LANES = 128
SUBS = 8
EPS = 1e-06
F32 = jnp.float32
BF16 = jnp.bfloat16
MESH = pl.DeviceIdType.MESH


def log2(n):
    assert n & (n - 1) == 0
    return n.bit_length() - 1


def div(x, n):
    return lax.shift_right_logical(x, jnp.int32(log2(n)))


def mod(x, n):
    return x & (n - 1)


def iota(shape, dim):
    return lax.broadcasted_iota(jnp.int32, shape, dim)


def dot(a, b, dims=((1,), (0,))):
    return lax.dot_general(a, b, (dims, ((), ())), preferred_element_type=F32)


def loop(count, body):
    if count <= 8:
        for k in range(count):
            body(k)
    else:

        def step(k, carry):
            body(k)
            return carry

        lax.fori_loop(0, count, step, 0)


def kernel(
    nb, nr, pairs,
    q_ref, pos_ref, pair_ref, code_ref, book_ref,
    loss_ref, qgrad_ref, pgrad_ref, cgrad_ref,
    info, pair_unit, own_unit, own_inv, own_codes, send2, recv2, sums, blocks, total, send4, recv4,
    info_send, info_recv, s2, r2, s3, f3, r3, s4, r4,
):
    me_b = lax.axis_index("blk")
    me_r = lax.axis_index("rep")
    me = me_b * nr + me_r
    nd = nb * nr
    books = code_ref.shape[0]
    feat = q_ref.shape[1]
    rows = q_ref.shape[0]
    span = pairs * PR
    own_rows = PBLK_DEV * PR

    codes = code_ref[...].astype(F32).astype(BF16)
    lane = iota((own_rows, LANES), 1)
    sub = iota((own_rows, LANES), 0)
    keep = iota((books, LANES), 0) == div(iota((books, LANES), 1), PR)
    sub8 = iota((SUBS, LANES), 0)
    mine = jnp.zeros((SUBS, LANES), F32)
    for j in range(PBLK_DEV):
        shift = (sub == j * PR + mod(lane, PR)).astype(BF16)
        line = jnp.sum(jnp.where(keep, dot(codes, shift), 0.0), axis=0, keepdims=True)
        mine = jnp.where(sub8 == j, line, mine)
    spread = (iota((pairs, LANES), 0) == iota((pairs, LANES), 1)).astype(BF16)
    pair_line = dot(jnp.broadcast_to(pair_ref[...].astype(F32), (SUBS, pairs)).astype(BF16), spread)
    mine = jnp.where(sub8 == PBLK_DEV, pair_line, mine)
    info[me] = mine

    def tell(k, carry):
        to = lax.rem(me + k, nd)
        pltpu.make_async_remote_copy(
            src_ref=info.at[me], dst_ref=info.at[me],
            send_sem=info_send, recv_sem=info_recv,
            device_id={"blk": to // nr, "rep": lax.rem(to, nr)}, device_id_type=MESH,
        ).start()
        return carry

    lax.fori_loop(1, nd, tell, 0)
    everyone = info.at[pl.ds(0, nd - 1)]
    pltpu.make_async_copy(everyone, everyone, info_recv).wait()

    heard = info[...].reshape(nd * SUBS, LANES).astype(BF16)
    chunk = min(32, nb * PBLK_DEV, nr * pairs)
    tall = chunk * PR
    pair_row = mine[PBLK_DEV : PBLK_DEV + 1, :]
    grow = (div(iota((tall, chunk), 0), PR) == iota((tall, chunk), 1)).astype(BF16)
    in_row = mod(iota((tall, LANES), 0), PR) == mod(iota((tall, LANES), 1), PR)
    code_line = iota((1, CODES), 1).astype(F32)
    wide = iota((chunk, nd * SUBS), 1)
    from_dev = div(wide, SUBS)
    from_row = mod(wide, SUBS)

    def code_of(spread_codes, book):
        pick = (div(iota((LANES, CODES), 0), PR) == book).astype(BF16)
        return dot(spread_codes, pick)

    def embed(select):
        picked = dot(select.astype(BF16), heard)
        spread_codes = jnp.where(in_row, dot(grow, picked.astype(BF16)), 0.0).astype(BF16)
        quant = jnp.zeros((tall, feat), F32)
        for k in range(books):
            onehot = (code_of(spread_codes, k) == code_line).astype(BF16)
            quant = quant + dot(onehot, book_ref[pl.ds(k * CODES, CODES), :])
        inverse = lax.rsqrt(jnp.sum(quant * quant, axis=1, keepdims=True) + EPS)
        return spread_codes, quant * inverse, inverse

    def pair_chunk(c):
        row = iota((chunk, 1), 0) + c * chunk
        slot = mod(row, pairs)
        rep = div(row, pairs)
        block = jnp.sum(
            jnp.where(iota((chunk, LANES), 1) == slot, pair_row, 0.0), axis=1, keepdims=True
        ).astype(jnp.int32)
        select = (
            (div(from_dev, nr) * PBLK_DEV + from_row == block)
            & (from_row < PBLK_DEV)
            & (mod(from_dev, nr) == rep)
        )
        unused, unit, inverse = embed(select)
        pair_unit[pl.ds(c * tall, tall), :] = unit.astype(BF16)

    loop(nr * pairs // chunk, pair_chunk)

    repeat = (iota((LANES, span), 0) == div(iota((LANES, span), 1), PR)).astype(BF16)
    my_blocks = dot(jnp.broadcast_to(pair_row, (SUBS, LANES)).astype(BF16), repeat)[0:1, :]
    inner = mod(iota((1, span), 1), PR).astype(F32)
    column_ids = jnp.concatenate(
        [my_blocks * (PR * nr) + (inner + r * PR) for r in range(nr)], axis=1
    )
    eye = iota((rows, rows), 0) == iota((rows, rows), 1)
    goal = jnp.sum(
        jnp.where(eye, pos_ref[pl.ds(me_r, 1), :].astype(F32), 0.0), axis=1, keepdims=True
    )
    query = q_ref[...]
    unit_bf = pair_unit[...]
    scores = dot(query, unit_bf, ((1,), (1,)))
    hit = column_ids == goal
    peak = jnp.max(scores, axis=1, keepdims=True)
    lse = peak + jnp.log(jnp.sum(jnp.exp(scores - peak), axis=1, keepdims=True))
    target = jnp.sum(jnp.where(hit, scores, 0.0), axis=1, keepdims=True)
    weight = (jnp.exp(scores - lse) - hit.astype(F32)).astype(BF16)
    grad_cols = dot(weight, query, ((0,), (0,)))
    send2[...] = grad_cols.astype(BF16).reshape(nr, span, feat)
    moves2 = []
    for d in range(nr - 1, 0, -1):
        to = lax.rem(me_r + d, nr)
        move = pltpu.make_async_remote_copy(
            src_ref=send2.at[to], dst_ref=recv2.at[d], send_sem=s2.at[d], recv_sem=r2.at[d],
            device_id={"blk": me_b, "rep": to}, device_id_type=MESH,
        )
        move.start()
        moves2.append(move)
    loss_ref[...] = jnp.sum(jnp.where(eye, lse - target, 0.0), axis=0, keepdims=True)
    qgrad_ref[...] = dot(weight, unit_bf)

    def own_chunk(c):
        row = iota((chunk, 1), 0) + c * chunk
        select = (from_dev == div(row, PBLK_DEV) * nr + me_r) & (from_row == mod(row, PBLK_DEV))
        spread_codes, unit, inverse = embed(select)
        own_unit[pl.ds(c * tall, tall), :] = unit
        own_inv[pl.ds(c * tall, tall), :] = jnp.broadcast_to(inverse, (tall, LANES))
        own_codes[pl.ds(c * tall, tall), :] = spread_codes

    loop(nb * PBLK_DEV // chunk, own_chunk)
    directory = jnp.concatenate(
        [info[b * nr][PBLK_DEV : PBLK_DEV + 1, :] for b in range(nb)], axis=0
    )
    blocks[...] = dot(directory.astype(BF16), repeat)

    for move in moves2:
        move.wait()
    summed = send2[me_r].astype(F32)
    for d in range(1, nr):
        summed = summed + recv2[d].astype(F32)
    sums[me_b] = summed.astype(BF16)

    peer = me_b + 1 - 2 * lax.rem(me_b, 2)
    half = nb // 2

    def share(slot, to, send_sem):
        return pltpu.make_async_remote_copy(
            src_ref=sums.at[slot], dst_ref=sums.at[slot], send_sem=send_sem,
            recv_sem=r3.at[slot], device_id={"blk": to, "rep": me_r}, device_id_type=MESH,
        )

    def add_block(b):
        line = blocks[pl.ds(b, 1), :].astype(jnp.int32)
        part = sums[b]

        def rows_chunk(c):
            row = iota((tall, span), 0) + c * tall
            select = (div(row, PR) == line) & (mod(row, PR) == mod(iota((tall, span), 1), PR))
            total[pl.ds(c * tall, tall), :] += dot(select.astype(BF16), part)

        loop(nb * PBLK_DEV // chunk, rows_chunk)

    share(me_b, peer, s3.at[0]).start()
    loop(half - 1, lambda k: share(me_b, lax.rem(me_b + 2 * (k + 1), nb), s3.at[k + 1]).start())
    total[...] = jnp.zeros_like(total)
    add_block(me_b)

    def pass_on(k):
        slot = lax.rem(me_b + nb - 2 * (k + 1), nb)
        share(slot, peer, f3.at[k]).wait_recv()
        share(slot, peer, f3.at[k]).start()
        add_block(slot)

    loop(half - 1, pass_on)

    def take(k):
        slot = lax.rem(peer + nb - 2 * k, nb)
        share(slot, peer, s3.at[0]).wait_recv()
        add_block(slot)

    loop(half, take)

    unit = own_unit[...]
    grad = total[...]
    grad = own_inv[:, 0:1] * (grad - unit * jnp.sum(unit * grad, axis=1, keepdims=True))
    total[...] = grad
    pgrad_ref[...] = total[pl.ds(me_b * own_rows, own_rows), :]

    group = send4.shape[0] * send4.shape[1]
    first = me_b * group
    wanted = code_of(own_codes[...], first // CODES)[:, 0:group]
    member = wanted == (iota((1, group), 1) + lax.rem(first, CODES)).astype(F32)
    part = dot(member.astype(BF16), grad.astype(BF16), ((0,), (0,)))
    send4[...] = part.astype(BF16).reshape(send4.shape)
    moves4 = []
    for d in range(nr - 1, 0, -1):
        to = lax.rem(me_r + d, nr)
        move = pltpu.make_async_remote_copy(
            src_ref=send4.at[to], dst_ref=recv4.at[d], send_sem=s4.at[d], recv_sem=r4.at[d],
            device_id={"blk": me_b, "rep": to}, device_id_type=MESH,
        )
        move.start()
        moves4.append(move)
    pltpu.make_async_copy(everyone, everyone, info_send).wait()
    loop(half, lambda k: share(me_b, peer, s3.at[k]).wait_send())
    loop(half - 1, lambda k: share(me_b, peer, f3.at[k]).wait_send())
    for move in moves4:
        move.wait()
    summed = send4[me_r].astype(F32)
    for d in range(1, nr):
        summed = summed + recv4[d].astype(F32)
    cgrad_ref[...] = summed


def shards(query_embed, positive_ids, pair_blocks, code_ids, codebooks):
    nb = lax.axis_size("blk")
    nr = lax.axis_size("rep")
    rows, feat = query_embed.shape[2:]
    pairs = pair_blocks.shape[1]
    books = code_ids.shape[2]
    share_rows = codebooks.shape[0] // (nb * nr)
    span = pairs * PR
    passages = nb * PBLK_DEV * PR
    assert books * PR == LANES and codebooks.shape[0] == books * CODES and pairs <= LANES
    assert CODES % (share_rows * nr) == 0 and nb * PBLK_DEV <= 256 and CODES <= 256
    vmem = pl.BlockSpec(memory_space=pltpu.VMEM)
    dma = pltpu.SemaphoreType.DMA
    outs = pl.pallas_call(
        functools.partial(kernel, nb, nr, pairs),
        out_shape=(
            jax.ShapeDtypeStruct((1, rows), F32),
            jax.ShapeDtypeStruct((rows, feat), F32),
            jax.ShapeDtypeStruct((PBLK_DEV * PR, feat), F32),
            jax.ShapeDtypeStruct((share_rows, feat), F32),
        ),
        in_specs=[vmem] * 5,
        out_specs=(vmem,) * 4,
        scratch_shapes=[
            pltpu.VMEM((nb * nr, SUBS, LANES), F32),
            pltpu.VMEM((nr * span, feat), BF16),
            pltpu.VMEM((passages, feat), F32),
            pltpu.VMEM((passages, LANES), F32),
            pltpu.VMEM((passages, LANES), BF16),
            pltpu.VMEM((nr, span, feat), BF16),
            pltpu.VMEM((nr, span, feat), BF16),
            pltpu.VMEM((nb, span, feat), BF16),
            pltpu.VMEM((nb, span), F32),
            pltpu.VMEM((passages, feat), F32),
            pltpu.VMEM((nr, share_rows, feat), BF16),
            pltpu.VMEM((nr, share_rows, feat), BF16),
            dma, dma, dma((nr,)), dma((nr,)),
            dma((nb // 2,)), dma((nb // 2,)), dma((nb,)), dma((nr,)), dma((nr,)),
        ],
        compiler_params=pltpu.CompilerParams(
            has_side_effects=True, vmem_limit_bytes=67_000_000
        ),
    )(query_embed[0, 0], positive_ids[0], pair_blocks, code_ids[0, 0], codebooks)
    loss, query_grad, passage_grad, codebook_grad = outs
    return (loss[None], query_grad[None, None], passage_grad[None, None], codebook_grad)


def solution(mesh):
    placed = (
        P("blk", "rep", None, None),
        P("blk", None, None),
        P("blk", None),
        P("blk", "rep", None, None),
        P(),
    )
    return jax.shard_map(
        shards,
        mesh=mesh,
        in_specs=placed,
        out_specs=(
            P("blk", "rep", None),
            P("blk", "rep", None, None),
            P("blk", "rep", None, None),
            P(("blk", "rep"), None),
        ),
        check_vma=False,
    )
```

time: 237 us -> 44.3 us (0.19)
  waiting for transfers between devices: 149 us -> 0 us
  blocking collectives: 45.4 us -> 0 us
  Pallas kernels: 0 us -> 39 us
  between operations: 14.4 us -> 0.65 us
  starting transfers between devices: 9.33 us -> 0 us
  matrix products: 6.19 us -> 0 us
  local copies, waits for them, and re-layouts: 10.3 us -> 4.42 us
    reduce_scatter x2 -> x0, waiting for transfers between devices: 145 us -> none  [the longest x1 141 us: shards(): lax.psum_scatter(jnp.dot(member, passage_grad, precision=lax.Precision.HI...]
    all_gather x5 -> x0, blocking collectives: 45.4 us -> none  [the longest x1 22.6 us: shards(): directory = lax.all_gather(pair_blocks, 'blk', axis=0, tiled=True)]
    pallas_call x0 -> x1, Pallas kernels: none -> 39 us  [shards(): pl.pallas_call(functools.partial(kernel, nb, nr, pairs), out_shape=(jax.S...]
    all_to_all x2 -> x0, starting transfers between devices: 9.25 us -> none  [the longest x1 5.88 us: shards(): lax.all_to_all(backward.reshape(owner_count, CAP, PR, feat_count), 'blk',...]
    dot_general x7 -> x0, matrix products: 6.19 us -> none  [the longest x1 3.31 us: shards(): jnp.dot(member, passage_grad, precision=lax.Precision.HIGHEST)]
    gather x2 -> x0, local copies, waits for them, and re-layouts: 6.01 us -> none  [the longest x1 5.46 us: shards(): picked = jnp.take(local_codes, book_of, axis=0)]
    unnamed x14 -> x10, local copies, waits for them, and re-layouts: 0.04 us -> 4.42 us
    all_to_all x2 -> x0, waiting for transfers between devices: 3.85 us -> none  [the longest x1 3.85 us: shards(): lax.all_to_all(backward.reshape(owner_count, CAP, PR, feat_count), 'blk',...]
  transfers between devices with their start and end apart: 4 -> 0, of which waited for: 3 -> 0; matrix products, arithmetic and copies ran while one was open for 5% -> 0% of each run, Pallas kernels for 0% -> 0%
where the time goes in v1:
time: 44.3 us; the launch traced here: 44 us
  Pallas kernels  39 us (88%)
  local copies, waits for them, and re-layouts  4.42 us (10%)
  between operations  0.65 us (1%)
    pallas_call x1, Pallas kernels, shards(): pl.pallas_call(functools.partial(kernel, nb, nr, pairs), out_shape=(jax.S...  39 us
    unnamed x10, local copies, waits for them, and re-layouts  4.42 us

profile of v1, /device:TPU:0, one launch (start us, length us, event | category | flops | bytes accessed | tf_op | source)
XLA Modules:
  0.0 44.0 jit_solution(15976546305134089225)
XLA Ops:
  0.6 39.0 %shard_map.84 = (f32[1,256]{1,0:T(1,128)}, f32[256,256]{1,0:T(8,128)}, f32[64,256]{1,0:T(8,128)}, f32[64,256]{1,0:T(8,128)}) custom-call(bf16[256,256]{1,0:T(8,128)(2,1)} %bitcast.7, s32[4,256]{1,0:T(4,128)} %bitcast.9, s32[1,8]{1,0:T(1,128)} %pair_ref.1, s32[8,64]{1,0:T(8,128)} %bitcast.10, bf16[2048,256]{1,0:T(8,128)(2,1)} %book_ref.1), custom_call_target="tpu_custom_call" | custom-call | tf_op jit(solution)/shard_map/pallas_call | solution.py:280
  39.6 0.0 copy-start.2
  39.6 0.7 %copy-done.2 = f32[1,256]{1,0:T(1,128)S(1)} copy-done((f32[1,256]{1,0:T(1,128)S(1)}, f32[1,256]{1,0:T(1,128)}, u32[]{:S(2)}) %copy-start.2) | copy-done | bytes 1048
  40.3 0.6 %copy.13 = f32[1,1,256]{2,1,0:T(1,128)} copy(f32[1,1,256]{2,1,0:T(1,128)S(1)} %bitcast.11) | data formatting | bytes 2048
  40.8 0.0 copy-start.1
  40.8 1.7 %copy.14 = f32[1,1,256,256]{3,2,1,0:T(8,128)} copy(f32[1,1,256,256]{3,2,1,0:T(8,128)} %bitcast.6) | data formatting | bytes 524288
  42.5 0.0 copy-done.1
  42.5 0.0 copy-start
  42.5 0.6 %copy.15 = f32[1,1,64,256]{3,2,1,0:T(8,128)} copy(f32[1,1,64,256]{3,2,1,0:T(8,128)S(1)} %bitcast.8) | data formatting | bytes 131072
  43.2 0.2 copy-done
  43.4 0.6 %copy.16 = f32[64,256]{1,0:T(8,128)} copy(f32[64,256]{1,0:T(8,128)S(1)} %copy-done) | data formatting | bytes 131072
Async XLA Ops:
  39.6 0.7 %copy-start.2 = (f32[1,256]{1,0:T(1,128)S(1)}, f32[1,256]{1,0:T(1,128)}, u32[]{:S(2)}) copy-start(f32[1,256]{1,0:T(1,128)} %get-tuple-element.8) | copy-start | bytes 3076
  40.8 1.7 %copy-start.1 = (f32[64,256]{1,0:T(8,128)S(1)}, f32[64,256]{1,0:T(8,128)}, u32[]{:S(2)}) copy-start(f32[64,256]{1,0:T(8,128)} %get-tuple-element.10) | copy-start | bytes 196612
  42.5 0.9 %copy-start = (f32[64,256]{1,0:T(8,128)S(1)}, f32[64,256]{1,0:T(8,128)}, u32[]{:S(2)}) copy-start(f32[64,256]{1,0:T(8,128)} %get-tuple-element.19) | copy-start | bytes 196612

commit v2 on v1

--- a/solution.py
+++ b/solution.py
@@ -57,12 +57,23 @@
     q_ref, pos_ref, pair_ref, code_ref, book_ref,
     loss_ref, qgrad_ref, pgrad_ref, cgrad_ref,
     info, pair_unit, own_unit, own_inv, own_codes, send2, recv2, sums, blocks, total, send4, recv4,
-    info_send, info_recv, s2, r2, s3, f3, r3, s4, r4,
+    blk_send, blk_recv, rep_send, rep_recv, s2, r2, s3, f3, r3, s4, r4,
 ):
     me_b = lax.axis_index("blk")
     me_r = lax.axis_index("rep")
-    me = me_b * nr + me_r
-    nd = nb * nr
+    barrier = pltpu.get_barrier_semaphore()
+    for d in range(1, nr):
+        pl.semaphore_signal(
+            barrier, inc=1, device_id={"blk": me_b, "rep": lax.rem(me_r + d, nr)},
+            device_id_type=MESH,
+        )
+    loop(
+        nb - 1,
+        lambda k: pl.semaphore_signal(
+            barrier, inc=1, device_id={"blk": lax.rem(me_b + k + 1, nb), "rep": me_r},
+            device_id_type=MESH,
+        ),
+    )
     books = code_ref.shape[0]
     feat = q_ref.shape[1]
     rows = q_ref.shape[0]
@@ -82,37 +93,42 @@
     spread = (iota((pairs, LANES), 0) == iota((pairs, LANES), 1)).astype(BF16)
     pair_line = dot(jnp.broadcast_to(pair_ref[...].astype(F32), (SUBS, pairs)).astype(BF16), spread)
     mine = jnp.where(sub8 == PBLK_DEV, pair_line, mine)
-    info[me] = mine
-
-    def tell(k, carry):
-        to = lax.rem(me + k, nd)
-        pltpu.make_async_remote_copy(
-            src_ref=info.at[me], dst_ref=info.at[me],
-            send_sem=info_send, recv_sem=info_recv,
-            device_id={"blk": to // nr, "rep": lax.rem(to, nr)}, device_id_type=MESH,
-        ).start()
-        return carry
-
-    lax.fori_loop(1, nd, tell, 0)
-    everyone = info.at[pl.ds(0, nd - 1)]
-    pltpu.make_async_copy(everyone, everyone, info_recv).wait()
-
-    heard = info[...].reshape(nd * SUBS, LANES).astype(BF16)
+    info[me_r, me_b] = mine
+    pl.semaphore_wait(barrier, nr - 1 + nb - 1)
+
+    def tell_blk(to):
+        return pltpu.make_async_remote_copy(
+            src_ref=info.at[me_r, me_b], dst_ref=info.at[me_r, me_b],
+            send_sem=blk_send, recv_sem=blk_recv,
+            device_id={"blk": to, "rep": me_r}, device_id_type=MESH,
+        )
+
+    def tell_rep(to):
+        return pltpu.make_async_remote_copy(
+            src_ref=info.at[me_r], dst_ref=info.at[me_r],
+            send_sem=rep_send, recv_sem=rep_recv,
+            device_id={"blk": me_b, "rep": to}, device_id_type=MESH,
+        )
+
+    loop(nb - 1, lambda k: tell_blk(lax.rem(me_b + k + 1, nb)).start())
+    others_blk = info.at[0, pl.ds(0, nb - 1)]
+    others_rep = info.at[pl.ds(0, nr - 1)]
+    pltpu.make_async_copy(others_blk, others_blk, blk_recv).wait()
+    for d in range(nr - 1, 0, -1):
+        tell_rep(lax.rem(me_r + d, nr)).start()
+
     chunk = min(32, nb * PBLK_DEV, nr * pairs)
+    flat = nb * SUBS
     tall = chunk * PR
     pair_row = mine[PBLK_DEV : PBLK_DEV + 1, :]
     grow = (div(iota((tall, chunk), 0), PR) == iota((tall, chunk), 1)).astype(BF16)
     in_row = mod(iota((tall, LANES), 0), PR) == mod(iota((tall, LANES), 1), PR)
     code_line = iota((1, CODES), 1).astype(F32)
-    wide = iota((chunk, nd * SUBS), 1)
-    from_dev = div(wide, SUBS)
-    from_row = mod(wide, SUBS)
-
     def code_of(spread_codes, book):
         pick = (div(iota((LANES, CODES), 0), PR) == book).astype(BF16)
         return dot(spread_codes, pick)
 
-    def embed(select):
+    def embed(select, heard):
         picked = dot(select.astype(BF16), heard)
         spread_codes = jnp.where(in_row, dot(grow, picked.astype(BF16)), 0.0).astype(BF16)
         quant = jnp.zeros((tall, feat), F32)
@@ -122,6 +138,30 @@
         inverse = lax.rsqrt(jnp.sum(quant * quant, axis=1, keepdims=True) + EPS)
         return spread_codes, quant * inverse, inverse
 
+    heard_own = info[me_r].reshape(flat, LANES).astype(BF16)
+
+    def own_chunk(c):
+        row = iota((chunk, 1), 0) + c * chunk
+        wide = iota((chunk, flat), 1)
+        select = (div(wide, SUBS) == div(row, PBLK_DEV)) & (mod(wide, SUBS) == mod(row, PBLK_DEV))
+        spread_codes, unit, inverse = embed(select, heard_own)
+        own_unit[pl.ds(c * tall, tall), :] = unit
+        own_inv[pl.ds(c * tall, tall), :] = jnp.broadcast_to(inverse, (tall, LANES))
+        own_codes[pl.ds(c * tall, tall), :] = spread_codes
+
+    loop(nb * PBLK_DEV // chunk, own_chunk)
+    repeat = (iota((LANES, span), 0) == div(iota((LANES, span), 1), PR)).astype(BF16)
+    directory = jnp.concatenate(
+        [info[me_r, b][PBLK_DEV : PBLK_DEV + 1, :] for b in range(nb)], axis=0
+    )
+    blocks[...] = dot(directory.astype(BF16), repeat)
+
+    pltpu.make_async_copy(others_rep, others_rep, rep_recv).wait()
+    heard = info[...].reshape(nr * flat, LANES).astype(BF16)
+    wide = iota((chunk, nr * flat), 1)
+    from_dev = div(wide, SUBS)
+    from_row = mod(wide, SUBS)
+
     def pair_chunk(c):
         row = iota((chunk, 1), 0) + c * chunk
         slot = mod(row, pairs)
@@ -130,16 +170,15 @@
             jnp.where(iota((chunk, LANES), 1) == slot, pair_row, 0.0), axis=1, keepdims=True
         ).astype(jnp.int32)
         select = (
-            (div(from_dev, nr) * PBLK_DEV + from_row == block)
+            (mod(from_dev, nb) * PBLK_DEV + from_row == block)
             & (from_row < PBLK_DEV)
-            & (mod(from_dev, nr) == rep)
-        )
-        unused, unit, inverse = embed(select)
+            & (div(from_dev, nb) == rep)
+        )
+        unused, unit, inverse = embed(select, heard)
         pair_unit[pl.ds(c * tall, tall), :] = unit.astype(BF16)
 
     loop(nr * pairs // chunk, pair_chunk)
 
-    repeat = (iota((LANES, span), 0) == div(iota((LANES, span), 1), PR)).astype(BF16)
     my_blocks = dot(jnp.broadcast_to(pair_row, (SUBS, LANES)).astype(BF16), repeat)[0:1, :]
     inner = mod(iota((1, span), 1), PR).astype(F32)
     column_ids = jnp.concatenate(
@@ -171,20 +210,6 @@
     loss_ref[...] = jnp.sum(jnp.where(eye, lse - target, 0.0), axis=0, keepdims=True)
     qgrad_ref[...] = dot(weight, unit_bf)
 
-    def own_chunk(c):
-        row = iota((chunk, 1), 0) + c * chunk
-        select = (from_dev == div(row, PBLK_DEV) * nr + me_r) & (from_row == mod(row, PBLK_DEV))
-        spread_codes, unit, inverse = embed(select)
-        own_unit[pl.ds(c * tall, tall), :] = unit
-        own_inv[pl.ds(c * tall, tall), :] = jnp.broadcast_to(inverse, (tall, LANES))
-        own_codes[pl.ds(c * tall, tall), :] = spread_codes
-
-    loop(nb * PBLK_DEV // chunk, own_chunk)
-    directory = jnp.concatenate(
-        [info[b * nr][PBLK_DEV : PBLK_DEV + 1, :] for b in range(nb)], axis=0
-    )
-    blocks[...] = dot(directory.astype(BF16), repeat)
-
     for move in moves2:
         move.wait()
     summed = send2[me_r].astype(F32)
@@ -253,7 +278,8 @@
         )
         move.start()
         moves4.append(move)
-    pltpu.make_async_copy(everyone, everyone, info_send).wait()
+    pltpu.make_async_copy(others_blk, others_blk, blk_send).wait()
+    pltpu.make_async_copy(others_rep, others_rep, rep_send).wait()
     loop(half, lambda k: share(me_b, peer, s3.at[k]).wait_send())
     loop(half - 1, lambda k: share(me_b, peer, f3.at[k]).wait_send())
     for move in moves4:
@@ -262,6 +288,15 @@
     for d in range(1, nr):
         summed = summed + recv4[d].astype(F32)
     cgrad_ref[...] = summed
+
+
+def write_out(*refs):
+    sems = refs[8]
+    moves = [pltpu.make_async_copy(refs[k], refs[k + 4], sems.at[k]) for k in range(4)]
+    for move in moves:
+        move.start()
+    for move in moves:
+        move.wait()
 
 
 def shards(query_embed, positive_ids, pair_blocks, code_ids, codebooks):
@@ -276,19 +311,22 @@
     assert books * PR == LANES and codebooks.shape[0] == books * CODES and pairs <= LANES
     assert CODES % (share_rows * nr) == 0 and nb * PBLK_DEV <= 256 and CODES <= 256
     vmem = pl.BlockSpec(memory_space=pltpu.VMEM)
+    hbm = pl.BlockSpec(memory_space=pltpu.HBM)
     dma = pltpu.SemaphoreType.DMA
+    limit = 67_000_000 if nb * span * feat > 8_000_000 else 32_000_000
+    shapes = (
+        jax.ShapeDtypeStruct((1, rows), F32),
+        jax.ShapeDtypeStruct((rows, feat), F32),
+        jax.ShapeDtypeStruct((PBLK_DEV * PR, feat), F32),
+        jax.ShapeDtypeStruct((share_rows, feat), F32),
+    )
     outs = pl.pallas_call(
         functools.partial(kernel, nb, nr, pairs),
-        out_shape=(
-            jax.ShapeDtypeStruct((1, rows), F32),
-            jax.ShapeDtypeStruct((rows, feat), F32),
-            jax.ShapeDtypeStruct((PBLK_DEV * PR, feat), F32),
-            jax.ShapeDtypeStruct((share_rows, feat), F32),
-        ),
+        out_shape=shapes,
         in_specs=[vmem] * 5,
         out_specs=(vmem,) * 4,
         scratch_shapes=[
-            pltpu.VMEM((nb * nr, SUBS, LANES), F32),
+            pltpu.VMEM((nr, nb, SUBS, LANES), F32),
             pltpu.VMEM((nr * span, feat), BF16),
             pltpu.VMEM((passages, feat), F32),
             pltpu.VMEM((passages, LANES), F32),
@@ -300,14 +338,21 @@
             pltpu.VMEM((passages, feat), F32),
             pltpu.VMEM((nr, share_rows, feat), BF16),
             pltpu.VMEM((nr, share_rows, feat), BF16),
-            dma, dma, dma((nr,)), dma((nr,)),
+            dma, dma, dma, dma, dma((nr,)), dma((nr,)),
             dma((nb // 2,)), dma((nb // 2,)), dma((nb,)), dma((nr,)), dma((nr,)),
         ],
         compiler_params=pltpu.CompilerParams(
-            has_side_effects=True, vmem_limit_bytes=67_000_000
+            has_side_effects=True, collective_id=0, vmem_limit_bytes=limit
         ),
     )(query_embed[0, 0], positive_ids[0], pair_blocks, code_ids[0, 0], codebooks)
-    loss, query_grad, passage_grad, codebook_grad = outs
+    loss, query_grad, passage_grad, codebook_grad = pl.pallas_call(
+        write_out,
+        out_shape=shapes,
+        in_specs=[vmem] * 4,
+        out_specs=(hbm,) * 4,
+        scratch_shapes=[dma((4,))],
+        compiler_params=pltpu.CompilerParams(vmem_limit_bytes=8_000_000),
+    )(*outs)
     return (loss[None], query_grad[None, None], passage_grad[None, None], codebook_grad)
 
 

time: 44.3 us -> 39.8 us (0.90)
  Pallas kernels: 39 us -> 35.5 us
  local copies, waits for them, and re-layouts: 4.42 us -> 3.49 us
    pallas_call x1 -> x2, Pallas kernels: 39 us -> 35.5 us  [the longest x1 34.7 us: shards(): pl.pallas_call(functools.partial(kernel, nb, nr, pairs), out_shape=shapes...]
    unnamed x10, local copies, waits for them, and re-layouts: 4.42 us -> 3.49 us
where the time goes in v2:
time: 39.8 us; the launch traced here: 39.6 us
  Pallas kernels  35.5 us (89%)
  local copies, waits for them, and re-layouts  3.49 us (9%)
  between operations  0.66 us (2%)
    pallas_call x1, Pallas kernels, shards(): pl.pallas_call(functools.partial(kernel, nb, nr, pairs), out_shape=shapes...  34.7 us
    unnamed x10, local copies, waits for them, and re-layouts  3.49 us

profile of v2, /device:TPU:0, one launch (start us, length us, event | category | flops | bytes accessed | tf_op | source)
XLA Modules:
  0.0 39.6 jit_solution(14849317730400300431)
XLA Ops:
  0.6 0.0 copy-start.2
  0.6 0.0 copy-start.4
  0.7 0.7 %copy-done.2 = s32[1,4,256]{2,1,0:T(4,128)S(1)} copy-done((s32[1,4,256]{2,1,0:T(4,128)S(1)}, s32[1,4,256]{2,1,0:T(4,128)}, u32[]{:S(2)}) %copy-start.2) | copy-done | bytes 4120
  1.3 0.0 copy-done.4
  1.3 0.0 copy-start
  1.3 1.2 %copy-done = bf16[2048,256]{1,0:T(8,128)(2,1)S(1)} copy-done((bf16[2048,256]{1,0:T(8,128)(2,1)S(1)}, bf16[2048,256]{1,0:T(8,128)(2,1)}, u32[]{:S(2)}) %copy-start) | copy-done | bytes 1048600
  2.5 0.0 copy-start.1
  2.6 0.9 %copy-done.1 = bf16[1,1,256,256]{3,2,1,0:T(8,128)(2,1)S(1)} copy-done((bf16[1,1,256,256]{3,2,1,0:T(8,128)(2,1)S(1)}, bf16[1,1,256,256]{3,2,1,0:T(8,128)(2,1)}, u32[]{:S(2)}) %copy-start.1) | copy-done | bytes 131096
  3.5 0.0 copy-start.3
  3.5 0.7 %copy-done.3 = s32[1,1,8,64]{3,2,1,0:T(8,128)S(1)} copy-done((s32[1,1,8,64]{3,2,1,0:T(8,128)S(1)}, s32[1,1,8,64]{3,2,1,0:T(8,128)}, u32[]{:S(2)}) %copy-start.3) | copy-done | bytes 2072
  4.1 34.7 %shard_map.84 = (f32[1,256]{1,0:T(1,128)S(1)}, f32[256,256]{1,0:T(8,128)S(1)}, f32[64,256]{1,0:T(8,128)S(1)}, f32[64,256]{1,0:T(8,128)S(1)}) custom-call(bf16[256,256]{1,0:T(8,128)(2,1)S(1)} %bitcast.6, s32[4,256]{1,0:T(4,128)S(1)} %bitcast.7, s32[1,8]{1,0:T(1,128)S(1)} %copy-done.4, s32[8,64]{1,0:T(8,128)S(1)} %bitcast.8, bf16[2048,256]{1,0:T(8,128)(2,1)S(1)} %copy-done), custom_call_target="tpu_custom_call" | custom-call | tf_op jit(solution)/shard_map/pallas_call | solution.py:323
  38.8 0.8 %shard_map.85 = (f32[1,256]{1,0:T(1,128)}, f32[256,256]{1,0:T(8,128)}, f32[64,256]{1,0:T(8,128)}, f32[64,256]{1,0:T(8,128)}) custom-call(f32[1,256]{1,0:T(1,128)S(1)} %get-tuple-element.12.refs_0_, f32[256,256]{1,0:T(8,128)S(1)} %get-tuple-element.13.refs_1_, f32[64,256]{1,0:T(8,128)S(1)} %get-tuple-element.14.refs_2_, f32[64,256]{1,0:T(8,128)S(1)} %get-tuple-element.15.refs_3_), custom_call_target="tpu_custom_call" | custom-call | tf_op jit(solution)/shard_map/pallas_call | solution.py:348
Async XLA Ops:
  0.6 0.7 %copy-start.2 = (s32[1,4,256]{2,1,0:T(4,128)S(1)}, s32[1,4,256]{2,1,0:T(4,128)}, u32[]{:S(2)}) copy-start(s32[1,4,256]{2,1,0:T(4,128)} %param.6) | copy-start | bytes 12292
  0.6 0.7 %copy-start.4 = (s32[1,8]{1,0:T(1,128)S(1)}, s32[1,8]{1,0:T(1,128)}, u32[]{:S(2)}) copy-start(s32[1,8]{1,0:T(1,128)} %pair_ref.1) | copy-start | bytes 100
  1.3 1.2 %copy-start = (bf16[2048,256]{1,0:T(8,128)(2,1)S(1)}, bf16[2048,256]{1,0:T(8,128)(2,1)}, u32[]{:S(2)}) copy-start(bf16[2048,256]{1,0:T(8,128)(2,1)} %book_ref.1) | copy-start | bytes 3145732
  2.5 0.9 %copy-start.1 = (bf16[1,1,256,256]{3,2,1,0:T(8,128)(2,1)S(1)}, bf16[1,1,256,256]{3,2,1,0:T(8,128)(2,1)}, u32[]{:S(2)}) copy-start(bf16[1,1,256,256]{3,2,1,0:T(8,128)(2,1)} %param.5) | copy-start | bytes 393220
  3.5 0.7 %copy-start.3 = (s32[1,1,8,64]{3,2,1,0:T(8,128)S(1)}, s32[1,1,8,64]{3,2,1,0:T(8,128)}, u32[]{:S(2)}) copy-start(s32[1,1,8,64]{3,2,1,0:T(8,128)} %param.8) | copy-start | bytes 6148

commit v3 on v2

--- a/solution.py
+++ b/solution.py
@@ -12,6 +12,7 @@
 PBLK_DEV = 4
 LANES = 128
 SUBS = 8
+PARTS = 2
 EPS = 1e-06
 F32 = jnp.float32
 BF16 = jnp.bfloat16
@@ -197,65 +198,78 @@
     target = jnp.sum(jnp.where(hit, scores, 0.0), axis=1, keepdims=True)
     weight = (jnp.exp(scores - lse) - hit.astype(F32)).astype(BF16)
     grad_cols = dot(weight, query, ((0,), (0,)))
-    send2[...] = grad_cols.astype(BF16).reshape(nr, span, feat)
+    width = feat // PARTS
+    for h in range(PARTS):
+        piece = grad_cols[:, h * width : (h + 1) * width].astype(BF16)
+        send2[h] = piece.reshape(nr, span, width)
     moves2 = []
-    for d in range(nr - 1, 0, -1):
-        to = lax.rem(me_r + d, nr)
-        move = pltpu.make_async_remote_copy(
-            src_ref=send2.at[to], dst_ref=recv2.at[d], send_sem=s2.at[d], recv_sem=r2.at[d],
-            device_id={"blk": me_b, "rep": to}, device_id_type=MESH,
-        )
-        move.start()
-        moves2.append(move)
+    for h in range(PARTS):
+        moves2.append([])
+        for d in range(nr - 1, 0, -1):
+            to = lax.rem(me_r + d, nr)
+            move = pltpu.make_async_remote_copy(
+                src_ref=send2.at[h, to], dst_ref=recv2.at[h, d],
+                send_sem=s2.at[h, d], recv_sem=r2.at[h, d],
+                device_id={"blk": me_b, "rep": to}, device_id_type=MESH,
+            )
+            move.start()
+            moves2[h].append(move)
     loss_ref[...] = jnp.sum(jnp.where(eye, lse - target, 0.0), axis=0, keepdims=True)
     qgrad_ref[...] = dot(weight, unit_bf)
 
-    for move in moves2:
-        move.wait()
-    summed = send2[me_r].astype(F32)
-    for d in range(1, nr):
-        summed = summed + recv2[d].astype(F32)
-    sums[me_b] = summed.astype(BF16)
-
     peer = me_b + 1 - 2 * lax.rem(me_b, 2)
     half = nb // 2
 
-    def share(slot, to, send_sem):
+    def share(h, slot, to, send_sem):
         return pltpu.make_async_remote_copy(
-            src_ref=sums.at[slot], dst_ref=sums.at[slot], send_sem=send_sem,
-            recv_sem=r3.at[slot], device_id={"blk": to, "rep": me_r}, device_id_type=MESH,
-        )
-
-    def add_block(b):
+            src_ref=sums.at[h, slot], dst_ref=sums.at[h, slot], send_sem=send_sem,
+            recv_sem=r3.at[h, slot], device_id={"blk": to, "rep": me_r}, device_id_type=MESH,
+        )
+
+    def add_block(h, b):
         line = blocks[pl.ds(b, 1), :].astype(jnp.int32)
-        part = sums[b]
+        part = sums[h, b]
 
         def rows_chunk(c):
             row = iota((tall, span), 0) + c * tall
             select = (div(row, PR) == line) & (mod(row, PR) == mod(iota((tall, span), 1), PR))
-            total[pl.ds(c * tall, tall), :] += dot(select.astype(BF16), part)
+            total[pl.ds(c * tall, tall), pl.ds(h * width, width)] += dot(select.astype(BF16), part)
 
         loop(nb * PBLK_DEV // chunk, rows_chunk)
 
-    share(me_b, peer, s3.at[0]).start()
-    loop(half - 1, lambda k: share(me_b, lax.rem(me_b + 2 * (k + 1), nb), s3.at[k + 1]).start())
     total[...] = jnp.zeros_like(total)
-    add_block(me_b)
-
-    def pass_on(k):
-        slot = lax.rem(me_b + nb - 2 * (k + 1), nb)
-        share(slot, peer, f3.at[k]).wait_recv()
-        share(slot, peer, f3.at[k]).start()
-        add_block(slot)
-
-    loop(half - 1, pass_on)
-
-    def take(k):
-        slot = lax.rem(peer + nb - 2 * k, nb)
-        share(slot, peer, s3.at[0]).wait_recv()
-        add_block(slot)
-
-    loop(half, take)
+    for h in range(PARTS):
+        for move in moves2[h]:
+            move.wait()
+        summed = send2[h, me_r].astype(F32)
+        for d in range(1, nr):
+            summed = summed + recv2[h, d].astype(F32)
+        sums[h, me_b] = summed.astype(BF16)
+        share(h, me_b, peer, s3.at[h, 0]).start()
+
+        def send_far(k):
+            share(h, me_b, lax.rem(me_b + 2 * (k + 1), nb), s3.at[h, k + 1]).start()
+
+        loop(half - 1, send_far)
+    for h in range(PARTS):
+        add_block(h, me_b)
+    for h in range(PARTS):
+
+        def pass_on(k):
+            slot = lax.rem(me_b + nb - 2 * (k + 1), nb)
+            share(h, slot, peer, f3.at[h, k]).wait_recv()
+            share(h, slot, peer, f3.at[h, k]).start()
+            add_block(h, slot)
+
+        loop(half - 1, pass_on)
+    for h in range(PARTS):
+
+        def take(k):
+            slot = lax.rem(peer + nb - 2 * k, nb)
+            share(h, slot, peer, s3.at[h, 0]).wait_recv()
+            add_block(h, slot)
+
+        loop(half, take)
 
     unit = own_unit[...]
     grad = total[...]
@@ -280,8 +294,9 @@
         moves4.append(move)
     pltpu.make_async_copy(others_blk, others_blk, blk_send).wait()
     pltpu.make_async_copy(others_rep, others_rep, rep_send).wait()
-    loop(half, lambda k: share(me_b, peer, s3.at[k]).wait_send())
-    loop(half - 1, lambda k: share(me_b, peer, f3.at[k]).wait_send())
+    for h in range(PARTS):
+        loop(half, lambda k: share(h, me_b, peer, s3.at[h, k]).wait_send())
+        loop(half - 1, lambda k: share(h, me_b, peer, f3.at[h, k]).wait_send())
     for move in moves4:
         move.wait()
     summed = send4[me_r].astype(F32)
@@ -331,15 +346,15 @@
             pltpu.VMEM((passages, feat), F32),
             pltpu.VMEM((passages, LANES), F32),
             pltpu.VMEM((passages, LANES), BF16),
-            pltpu.VMEM((nr, span, feat), BF16),
-            pltpu.VMEM((nr, span, feat), BF16),
-            pltpu.VMEM((nb, span, feat), BF16),
+            pltpu.VMEM((PARTS, nr, span, feat // PARTS), BF16),
+            pltpu.VMEM((PARTS, nr, span, feat // PARTS), BF16),
+            pltpu.VMEM((PARTS, nb, span, feat // PARTS), BF16),
             pltpu.VMEM((nb, span), F32),
             pltpu.VMEM((passages, feat), F32),
             pltpu.VMEM((nr, share_rows, feat), BF16),
             pltpu.VMEM((nr, share_rows, feat), BF16),
-            dma, dma, dma, dma, dma((nr,)), dma((nr,)),
-            dma((nb // 2,)), dma((nb // 2,)), dma((nb,)), dma((nr,)), dma((nr,)),
+            dma, dma, dma, dma, dma((PARTS, nr)), dma((PARTS, nr)),
+            dma((PARTS, nb // 2)), dma((PARTS, nb // 2)), dma((PARTS, nb)), dma((nr,)), dma((nr,)),
         ],
         compiler_params=pltpu.CompilerParams(
             has_side_effects=True, collective_id=0, vmem_limit_bytes=limit

time: 39.8 us -> 39.4 us (0.990)
  Pallas kernels: 35.5 us -> 35 us
    pallas_call x1, Pallas kernels: 34.7 us -> 34.2 us  [shards(): pl.pallas_call(functools.partial(kernel, nb, nr, pairs), out_shape=shapes...]
where the time goes in v3:
time: 39.4 us; the launch traced here: 39.2 us
  Pallas kernels  35 us (89%)
  local copies, waits for them, and re-layouts  3.49 us (9%)
  between operations  0.66 us (2%)
    pallas_call x1, Pallas kernels, shards(): pl.pallas_call(functools.partial(kernel, nb, nr, pairs), out_shape=shapes...  34.2 us
    unnamed x10, local copies, waits for them, and re-layouts  3.49 us

profile of v3, /device:TPU:0, one launch (start us, length us, event | category | flops | bytes accessed | tf_op | source)
XLA Modules:
  0.0 39.2 jit_solution(8265679273019395824)
XLA Ops:
  0.6 0.0 copy-start.2
  0.6 0.0 copy-start.4
  0.7 0.7 %copy-done.2 = s32[1,4,256]{2,1,0:T(4,128)S(1)} copy-done((s32[1,4,256]{2,1,0:T(4,128)S(1)}, s32[1,4,256]{2,1,0:T(4,128)}, u32[]{:S(2)}) %copy-start.2) | copy-done | bytes 4120
  1.3 0.0 copy-done.4
  1.3 0.0 copy-start
  1.3 1.2 %copy-done = bf16[2048,256]{1,0:T(8,128)(2,1)S(1)} copy-done((bf16[2048,256]{1,0:T(8,128)(2,1)S(1)}, bf16[2048,256]{1,0:T(8,128)(2,1)}, u32[]{:S(2)}) %copy-start) | copy-done | bytes 1048600
  2.5 0.0 copy-start.1
  2.6 0.9 %copy-done.1 = bf16[1,1,256,256]{3,2,1,0:T(8,128)(2,1)S(1)} copy-done((bf16[1,1,256,256]{3,2,1,0:T(8,128)(2,1)S(1)}, bf16[1,1,256,256]{3,2,1,0:T(8,128)(2,1)}, u32[]{:S(2)}) %copy-start.1) | copy-done | bytes 131096
  3.5 0.0 copy-start.3
  3.5 0.7 %copy-done.3 = s32[1,1,8,64]{3,2,1,0:T(8,128)S(1)} copy-done((s32[1,1,8,64]{3,2,1,0:T(8,128)S(1)}, s32[1,1,8,64]{3,2,1,0:T(8,128)}, u32[]{:S(2)}) %copy-start.3) | copy-done | bytes 2072
  4.1 34.2 %shard_map.84 = (f32[1,256]{1,0:T(1,128)S(1)}, f32[256,256]{1,0:T(8,128)S(1)}, f32[64,256]{1,0:T(8,128)S(1)}, f32[64,256]{1,0:T(8,128)S(1)}) custom-call(bf16[256,256]{1,0:T(8,128)(2,1)S(1)} %bitcast.6, s32[4,256]{1,0:T(4,128)S(1)} %bitcast.7, s32[1,8]{1,0:T(1,128)S(1)} %copy-done.4, s32[8,64]{1,0:T(8,128)S(1)} %bitcast.8, bf16[2048,256]{1,0:T(8,128)(2,1)S(1)} %copy-done), custom_call_target="tpu_custom_call" | custom-call | tf_op jit(solution)/shard_map/pallas_call | solution.py:338
  38.4 0.8 %shard_map.85 = (f32[1,256]{1,0:T(1,128)}, f32[256,256]{1,0:T(8,128)}, f32[64,256]{1,0:T(8,128)}, f32[64,256]{1,0:T(8,128)}) custom-call(f32[1,256]{1,0:T(1,128)S(1)} %get-tuple-element.12.refs_0_, f32[256,256]{1,0:T(8,128)S(1)} %get-tuple-element.13.refs_1_, f32[64,256]{1,0:T(8,128)S(1)} %get-tuple-element.14.refs_2_, f32[64,256]{1,0:T(8,128)S(1)} %get-tuple-element.15.refs_3_), custom_call_target="tpu_custom_call" | custom-call | tf_op jit(solution)/shard_map/pallas_call | solution.py:363
Async XLA Ops:
  0.6 0.7 %copy-start.2 = (s32[1,4,256]{2,1,0:T(4,128)S(1)}, s32[1,4,256]{2,1,0:T(4,128)}, u32[]{:S(2)}) copy-start(s32[1,4,256]{2,1,0:T(4,128)} %param.6) | copy-start | bytes 12292
  0.6 0.7 %copy-start.4 = (s32[1,8]{1,0:T(1,128)S(1)}, s32[1,8]{1,0:T(1,128)}, u32[]{:S(2)}) copy-start(s32[1,8]{1,0:T(1,128)} %pair_ref.1) | copy-start | bytes 100
  1.3 1.2 %copy-start = (bf16[2048,256]{1,0:T(8,128)(2,1)S(1)}, bf16[2048,256]{1,0:T(8,128)(2,1)}, u32[]{:S(2)}) copy-start(bf16[2048,256]{1,0:T(8,128)(2,1)} %book_ref.1) | copy-start | bytes 3145732
  2.5 0.9 %copy-start.1 = (bf16[1,1,256,256]{3,2,1,0:T(8,128)(2,1)S(1)}, bf16[1,1,256,256]{3,2,1,0:T(8,128)(2,1)}, u32[]{:S(2)}) copy-start(bf16[1,1,256,256]{3,2,1,0:T(8,128)(2,1)} %param.5) | copy-start | bytes 393220
  3.5 0.7 %copy-start.3 = (s32[1,1,8,64]{3,2,1,0:T(8,128)S(1)}, s32[1,1,8,64]{3,2,1,0:T(8,128)}, u32[]{:S(2)}) copy-start(s32[1,1,8,64]{3,2,1,0:T(8,128)} %param.8) | copy-start | bytes 6148
